TPU v7x, 128 devices: a whole 4x4x4 slice. The times are simulated.
128 devices in a mesh: lat: 16 (over z, x), lon: 4 (over y), lev: 2 (over core).
Axes of the slice: x: 4, y: 4, z: 4, core: 2. Of those that a mesh axis runs over, the one named last changes fastest.
Arguments:
- pressure: float32 [64, 256, 128, 128], P('lat', 'lon', 'lev'), may hold values from 0.2 to 1.8
- earlier: float32 [64, 256, 128, 128], P('lat', 'lon', 'lev'), may hold values from 0.2 to 1.8
- speed_square: float32 [64, 256, 128, 128], P('lat', 'lon', 'lev'), may hold values from 0.05 to 0.3
Outputs:
- pressure_end: float32 [64, 256, 128, 128], P('lat', 'lon', 'lev')
All inputs are finite; a program needn't handle non-finite values.
Results may differ from a plain program's by a relative error of at most 0.00002.
Values sent between devices are 32-bit elements.
A program may use at most 320 MiB of HBM per device.

v0:
```python
import jax
import jax.numpy as jnp
from jax import lax
from jax.sharding import PartitionSpec as P

STEPS = 4


def with_halo(array, sides, width):
    edges = {}
    for axis, dim in sides:
        devices, length = (lax.axis_size(axis), array.shape[dim])
        up = [(i, (i + 1) % devices) for i in range(devices - 1)]
        last = lax.slice_in_dim(array, length - width, length, axis=dim)
        leading = lax.slice_in_dim(array, 0, width, axis=dim)
        edges[dim] = (
            lax.ppermute(last, axis, up),
            lax.ppermute(leading, axis, [(b, a) for a, b in up]),
        )
    done = []
    for _, dim in sides:
        low, high = edges[dim]
        around = [(width, width) if d in done else (0, 0) for d in range(array.ndim)]
        array = jnp.concatenate([jnp.pad(low, around), array, jnp.pad(high, around)], axis=dim)
        done.append(dim)
    return array


def inner_cells(values, dims):
    for dim in dims:
        values = lax.slice_in_dim(values, 1, values.shape[dim] - 1, axis=dim)
    return values


def side_cells(values, dim, start, dims):
    others = [other for other in dims if other != dim]
    values = inner_cells(values, others)
    return lax.slice_in_dim(values, start, start + values.shape[dim] - 2, axis=dim)


def advance(padded, before, speed_square):
    middle = inner_cells(padded, (0, 1, 2))
    lower = [side_cells(padded, dim, 0, (0, 1, 2)) for dim in (0, 1, 2)]
    upper = [side_cells(padded, dim, 2, (0, 1, 2)) for dim in (0, 1, 2)]
    spread = lower[0] + upper[0] + lower[1] + upper[1] + lower[2] + upper[2] - 6.0 * middle
    return 2.0 * middle - before + speed_square * spread


def shards(pressure, earlier, speed_square):
    for step in range(STEPS):
        padded = with_halo(pressure, (("lat", 0), ("lon", 1), ("lev", 2)), 1)
        later = advance(padded, earlier, speed_square)
        earlier, pressure = (pressure, later)
    return pressure


def solution(mesh):
    return jax.shard_map(
        shards,
        mesh=mesh,
        in_specs=(
            P("lat", "lon", "lev", None),
            P("lat", "lon", "lev", None),
            P("lat", "lon", "lev", None),
        ),
        out_specs=P("lat", "lon", "lev", None),
        check_vma=False,
    )
```

profile of v0, /device:TPU:1, one launch (start us, length us, event | category | flops | bytes accessed | tf_op | source)
XLA Modules:
  0.0 334.6 jit_solution(710126678883513660)
XLA Ops:
  0.0 4.1 %fusion.51 = (f32[1,64,64,128]{3,2,1,0:T(8,128)}, f32[1,64,64,128]{3,2,1,0:T(8,128)S(1)}) fusion(f32[4,64,64,128]{3,2,1,0:T(8,128)} %param.3), kind=kLoop, calls=%fused_computation.120 | loop fusion | bytes 8388608 | tf_op jit(solution)/shard_map/slice | solution.py:15
  4.1 4.2 %collective-permute-start = (f32[1,64,64,128]{3,2,1,0:T(8,128)S(1)}, f32[1,64,64,128]{3,2,1,0:T(8,128)S(1)}, u32[]{:S(2)}, u32[]{:S(2)}) collective-permute-start(f32[1,64,64,128]{3,2,1,0:T(8,128)S(1)} %get-tuple-element.28), channel_id=1, source_target_pairs={{0,8},{8,16},{16,24},{24,32},{32,40},{40,48},{48,56},{56,64},{64,7... | collective-permute-start | bytes 6291464 | tf_op jit(solution)/shard_map/ppermute | solution.py:17
  8.3 1.3 collective-permute-start.1
  9.7 3.2 collective-permute-start.2
  12.9 1.3 collective-permute-start.3
  14.4 1.3 collective-permute-start.4
  15.7 3.2 collective-permute-start.5
  18.9 33.6 %collective-permute-done = f32[1,64,64,128]{3,2,1,0:T(8,128)S(1)} collective-permute-done((f32[1,64,64,128]{3,2,1,0:T(8,128)S(1)}, f32[1,64,64,128]{3,2,1,0:T(8,128)S(1)}, u32[]{:S(2)}, u32[]{:S(2)}) %collective-permute-start) | collective-permute-done | bytes 2097184 | tf_op jit(solution)/shard_map/ppermute | solution.py:17
  52.5 1.5 constant_dynamic-update-slice_fusion.2
  54.0 4.7 %constant_dynamic-update-slice_fusion.1 = f32[6,64,64,128]{3,2,1,0:T(8,128)} fusion(f32[6,64,64,128]{3,2,1,0:T(8,128)} %constant_dynamic-update-slice_fusion.2, f32[4,64,64,128]{3,2,1,0:T(8,128)S(1)} %copy-done), kind=kLoop, calls=%fused_computation.107 | loop fusion | bytes 16777216
  58.7 1.3 copy-done.1
  60.0 1.5 constant_dynamic-update-slice_fusion
  61.5 26.1 %fusion.34 = f32[4,64,64,128]{3,2,1,0:T(8,128)} fusion(f32[4,64,64,128]{3,2,1,0:T(8,128)S(1)} %bitcast.17, f32[4,64,1,128]{3,2,1,0:T(1,128)S(1)} %bitcast.22, f32[6,1,64,128]{3,2,1,0:T(8,128)S(1)} %pad.51, f32[6,64,64,128]{3,2,1,0:T(8,128)} %constant_dynamic-update-slice_fusion, f32[6,1,64,128]{3,2,1,0:T(8,128)S(1)} %pad.50, ...), kind=kLoop, calls=%fused_computation.89 | loop fusion | flops 56623104 | bytes 50987008 | tf_op jit(solution)/shard_map/add | solution.py:46
  87.6 2.5 fusion.47
  90.1 4.2 %collective-permute-start.6 = (f32[1,64,64,128]{3,2,1,0:T(8,128)S(1)}, f32[1,64,64,128]{3,2,1,0:T(8,128)S(1)}, u32[]{:S(2)}, u32[]{:S(2)}) collective-permute-start(f32[1,64,64,128]{3,2,1,0:T(8,128)S(1)} %get-tuple-element.19), channel_id=1, source_target_pairs={{0,8},{8,16},{16,24},{24,32},{32,40},{40,48},{48,56},{56,64},{64,7... | collective-permute-start | bytes 6291464 | tf_op jit(solution)/shard_map/ppermute | solution.py:17
  94.4 1.3 collective-permute-start.7
  95.7 1.0 fusion.48
  96.7 3.2 collective-permute-start.8
  99.9 1.3 collective-permute-start.9
  101.2 1.7 fusion.46
  102.9 1.3 collective-permute-start.10
  104.3 4.0 %collective-permute-start.11 = (f32[4,64,1,128]{3,1,2,0:T(8,128)S(1)}, f32[4,64,1,128]{3,1,2,0:T(8,128)S(1)}, u32[]{:S(2)}, u32[]{:S(2)}) collective-permute-start(f32[4,64,1,128]{3,1,2,0:T(8,128)S(1)} %bitcast.29), channel_id=1, source_target_pairs={{1,0},{3,2},{5,4},{7,6},{9,8},{11,10},{13,12},{15,14},{17,16},{19,... | collective-permute-start | bytes 393224 | tf_op jit(solution)/shard_map/ppermute | solution.py:18
  109.2 28.5 %collective-permute-done.6 = f32[1,64,64,128]{3,2,1,0:T(8,128)S(1)} collective-permute-done((f32[1,64,64,128]{3,2,1,0:T(8,128)S(1)}, f32[1,64,64,128]{3,2,1,0:T(8,128)S(1)}, u32[]{:S(2)}, u32[]{:S(2)}) %collective-permute-start.6) | collective-permute-done | bytes 2097184 | tf_op jit(solution)/shard_map/ppermute | solution.py:17
  137.7 4.1 %collective-permute-done.7 = f32[1,64,64,128]{3,2,1,0:T(8,128)} collective-permute-done((f32[1,64,64,128]{3,2,1,0:T(8,128)S(1)}, f32[1,64,64,128]{3,2,1,0:T(8,128)}, u32[]{:S(2)}, u32[]{:S(2)}) %collective-permute-start.7) | collective-permute-done | bytes 2097184 | tf_op jit(solution)/shard_map/ppermute | solution.py:18
  141.8 28.5 %fusion.24 = f32[4,64,64,128]{3,2,1,0:T(8,128)} fusion(f32[4,64,64,128]{3,2,1,0:T(8,128)} %param.5, f32[4,64,1,128]{3,2,1,0:T(1,128)S(1)} %bitcast.25, f32[6,1,64,128]{3,2,1,0:T(8,128)S(1)} %pad.55, f32[6,1,64,128]{3,2,1,0:T(8,128)S(1)} %pad.54, f32[1,64,64,128]{3,2,1,0:T(8,128)} %collective-permute-done.7, f32[4,64,64,128]{3,2,1,0:T(8,128)} %fusion.34, ...), kind=kLoop, calls=%fused_computation.61 | loop fusion | flops 73400320 | bytes 38404096 | tf_op jit(solution)/shard_map/add | solution.py:46
  170.3 2.5 fusion.44
  172.9 3.1 collective-permute-start.12
  176.0 1.3 collective-permute-start.13
  178.3 3.2 collective-permute-start.14
  181.5 1.3 collective-permute-start.15
  182.8 1.7 fusion.43
  184.5 1.3 collective-permute-start.16
  185.8 5.3 %collective-permute-start.17 = (f32[4,64,1,128]{3,1,2,0:T(8,128)S(1)}, f32[4,64,1,128]{3,1,2,0:T(8,128)S(1)}, u32[]{:S(2)}, u32[]{:S(2)}) collective-permute-start(f32[4,64,1,128]{3,1,2,0:T(8,128)S(1)} %bitcast.30), channel_id=1, source_target_pairs={{1,0},{3,2},{5,4},{7,6},{9,8},{11,10},{13,12},{15,14},{17,16},{19,... | collective-permute-start | bytes 393224 | tf_op jit(solution)/shard_map/ppermute | solution.py:18
  192.0 26.2 %collective-permute-done.12 = f32[1,64,64,128]{3,2,1,0:T(8,128)S(1)} collective-permute-done((f32[1,64,64,128]{3,2,1,0:T(8,128)S(1)}, f32[1,64,64,128]{3,2,1,0:T(8,128)S(1)}, u32[]{:S(2)}, u32[]{:S(2)}) %collective-permute-start.12) | collective-permute-done | bytes 2097184 | tf_op jit(solution)/shard_map/ppermute | solution.py:17
  218.2 6.5 %collective-permute-done.13 = f32[1,64,64,128]{3,2,1,0:T(8,128)} collective-permute-done((f32[1,64,64,128]{3,2,1,0:T(8,128)S(1)}, f32[1,64,64,128]{3,2,1,0:T(8,128)}, u32[]{:S(2)}, u32[]{:S(2)}) %collective-permute-start.13) | collective-permute-done | bytes 2097184 | tf_op jit(solution)/shard_map/ppermute | solution.py:18
  224.6 28.5 %fusion.14 = f32[4,64,64,128]{3,2,1,0:T(8,128)} fusion(f32[4,64,64,128]{3,2,1,0:T(8,128)} %param.5, f32[4,64,1,128]{3,2,1,0:T(1,128)S(1)} %bitcast.24, f32[6,1,64,128]{3,2,1,0:T(8,128)S(1)} %pad.59, f32[6,1,64,128]{3,2,1,0:T(8,128)S(1)} %pad.58, f32[1,64,64,128]{3,2,1,0:T(8,128)} %collective-permute-done.13, f32[4,64,64,128]{3,2,1,0:T(8,128)} %fusion.24, ...), kind=kLoop, calls=%fused_computation.33 | loop fusion | flops 73400320 | bytes 38404096 | tf_op jit(solution)/shard_map/add | solution.py:46
  253.1 2.5 fusion.41
  255.6 5.0 %collective-permute-start.18 = (f32[1,64,64,128]{3,2,1,0:T(8,128)S(1)}, f32[1,64,64,128]{3,2,1,0:T(8,128)S(1)}, u32[]{:S(2)}, u32[]{:S(2)}) collective-permute-start(f32[1,64,64,128]{3,2,1,0:T(8,128)S(1)} %get-tuple-element.7), channel_id=1, source_target_pairs={{0,8},{8,16},{16,24},{24,32},{32,40},{40,48},{48,56},{56,64},{64,7... | collective-permute-start | bytes 6291464 | tf_op jit(solution)/shard_map/ppermute | solution.py:17
  260.7 1.3 collective-permute-start.19
  263.0 3.2 collective-permute-start.20
  266.2 1.3 collective-permute-start.21
  267.5 1.7 fusion.40
  269.2 6.0 %collective-permute-start.23 = (f32[4,64,1,128]{3,1,2,0:T(8,128)S(1)}, f32[4,64,1,128]{3,1,2,0:T(8,128)S(1)}, u32[]{:S(2)}, u32[]{:S(2)}) collective-permute-start(f32[4,64,1,128]{3,1,2,0:T(8,128)S(1)} %bitcast.31), channel_id=1, source_target_pairs={{1,0},{3,2},{5,4},{7,6},{9,8},{11,10},{13,12},{15,14},{17,16},{19,... | collective-permute-start | bytes 393224 | tf_op jit(solution)/shard_map/ppermute | solution.py:18
  275.2 1.3 collective-permute-start.22
  276.6 1.9 collective-permute-done.22
  278.5 23.5 %collective-permute-done.18 = f32[1,64,64,128]{3,2,1,0:T(8,128)S(1)} collective-permute-done((f32[1,64,64,128]{3,2,1,0:T(8,128)S(1)}, f32[1,64,64,128]{3,2,1,0:T(8,128)S(1)}, u32[]{:S(2)}, u32[]{:S(2)}) %collective-permute-start.18) | collective-permute-done | bytes 2097184 | tf_op jit(solution)/shard_map/ppermute | solution.py:17
  302.0 4.1 %collective-permute-done.19 = f32[1,64,64,128]{3,2,1,0:T(8,128)} collective-permute-done((f32[1,64,64,128]{3,2,1,0:T(8,128)S(1)}, f32[1,64,64,128]{3,2,1,0:T(8,128)}, u32[]{:S(2)}, u32[]{:S(2)}) %collective-permute-start.19) | collective-permute-done | bytes 2097184 | tf_op jit(solution)/shard_map/ppermute | solution.py:18
  306.1 28.4 %fusion.4 = f32[4,64,64,128]{3,2,1,0:T(8,128)} fusion(f32[4,64,64,128]{3,2,1,0:T(8,128)} %param.5, f32[4,64,1,128]{3,2,1,0:T(1,128)S(1)} %bitcast.19, f32[6,1,64,128]{3,2,1,0:T(8,128)S(1)} %pad.63, f32[6,1,64,128]{3,2,1,0:T(8,128)S(1)} %pad.62, f32[1,64,64,128]{3,2,1,0:T(8,128)} %collective-permute-done.19, f32[4,64,64,128]{3,2,1,0:T(8,128)} %fusion.14, ...), kind=kLoop, calls=%fused_computation.5 | loop fusion | flops 73400320 | bytes 38404096 | tf_op jit(solution)/shard_map/add | solution.py:46
  (36 shorter events, 4.0 us)
Async XLA Ops:
  0.0 9.6 %copy-start = (f32[4,64,64,128]{3,2,1,0:T(8,128)S(1)}, f32[4,64,64,128]{3,2,1,0:T(8,128)}, u32[]{:S(2)}) copy-start(f32[4,64,64,128]{3,2,1,0:T(8,128)} %param.3) | copy-start | bytes 25165828
  4.1 48.4 %collective-permute-start = (f32[1,64,64,128]{3,2,1,0:T(8,128)S(1)}, f32[1,64,64,128]{3,2,1,0:T(8,128)S(1)}, u32[]{:S(2)}, u32[]{:S(2)}) collective-permute-start(f32[1,64,64,128]{3,2,1,0:T(8,128)S(1)} %get-tuple-element.28), channel_id=1, source_target_pairs={{0,8},{8,16},{16,24},{24,32},{32,40},{40,48},{48,56},{56,64},{64,7... | collective-permute-start | bytes 6291464 | tf_op jit(solution)/shard_map/ppermute | solution.py:17
  8.3 50.3 %collective-permute-start.1 = (f32[1,64,64,128]{3,2,1,0:T(8,128)}, f32[1,64,64,128]{3,2,1,0:T(8,128)S(1)}, u32[]{:S(2)}, u32[]{:S(2)}) collective-permute-start(f32[1,64,64,128]{3,2,1,0:T(8,128)} %get-tuple-element.27), channel_id=1, source_target_pairs={{8,0},{16,8},{24,16},{32,24},{40,32},{48,40},{56,48},{64,56},{72,6... | collective-permute-start | bytes 6291464 | tf_op jit(solution)/shard_map/ppermute | solution.py:18
  9.7 6.0 %collective-permute-start.2 = (f32[4,1,64,128]{3,2,1,0:T(8,128)S(1)}, f32[4,1,64,128]{3,2,1,0:T(8,128)S(1)}, u32[]{:S(2)}, u32[]{:S(2)}) collective-permute-start(f32[4,1,64,128]{3,2,1,0:T(8,128)S(1)} %get-tuple-element.25), channel_id=1, source_target_pairs={{0,2},{2,4},{4,6},{1,3},{3,5},{5,7},{8,10},{10,12},{12,14},{9,11},... | collective-permute-start | bytes 393224 | tf_op jit(solution)/shard_map/ppermute | solution.py:17
  12.9 6.0 %collective-permute-start.3 = (f32[4,1,64,128]{3,2,1,0:T(8,128)S(1)}, f32[4,1,64,128]{3,2,1,0:T(8,128)S(1)}, u32[]{:S(2)}, u32[]{:S(2)}) collective-permute-start(f32[4,1,64,128]{3,2,1,0:T(8,128)S(1)} %get-tuple-element.26), channel_id=1, source_target_pairs={{2,0},{4,2},{6,4},{3,1},{5,3},{7,5},{10,8},{12,10},{14,12},{11,9},... | collective-permute-start | bytes 393224 | tf_op jit(solution)/shard_map/ppermute | solution.py:18
  14.4 47.1 %collective-permute-start.4 = (f32[4,64,1,128]{3,1,2,0:T(8,128)S(1)}, f32[4,64,1,128]{3,1,2,0:T(8,128)S(1)}, u32[]{:S(2)}, u32[]{:S(2)}) collective-permute-start(f32[4,64,1,128]{3,1,2,0:T(8,128)S(1)} %bitcast.27), channel_id=1, source_target_pairs={{0,1},{2,3},{4,5},{6,7},{8,9},{10,11},{12,13},{14,15},{16,17},{18,... | collective-permute-start | bytes 393224 | tf_op jit(solution)/shard_map/ppermute | solution.py:17
  15.7 45.8 %collective-permute-start.5 = (f32[4,64,1,128]{3,1,2,0:T(8,128)S(1)}, f32[4,64,1,128]{3,1,2,0:T(8,128)S(1)}, u32[]{:S(2)}, u32[]{:S(2)}) collective-permute-start(f32[4,64,1,128]{3,1,2,0:T(8,128)S(1)} %bitcast.26), channel_id=1, source_target_pairs={{1,0},{3,2},{5,4},{7,6},{9,8},{11,10},{13,12},{15,14},{17,16},{19,... | collective-permute-start | bytes 393224 | tf_op jit(solution)/shard_map/ppermute | solution.py:18
  52.5 9.0 %slice-start = ((s8[8388608]{0:T(1024)(128)(4,1)}), s8[4194304]{0:T(1024)(128)(4,1)S(1)}, s32[]{:S(2)}) async-start(s8[8388608]{0:T(1024)(128)(4,1)} %bitcast.16), calls=%async_computation | async-start | bytes 8388608
  54.0 7.5 %slice-start.1 = ((s8[8388608]{0:T(1024)(128)(4,1)}), s8[4194304]{0:T(1024)(128)(4,1)S(1)}, s32[]{:S(2)}) async-start(s8[8388608]{0:T(1024)(128)(4,1)} %bitcast.16), calls=%async_computation.1 | async-start | bytes 8388608
  58.7 1.3 copy-start.1
  90.1 47.6 %collective-permute-start.6 = (f32[1,64,64,128]{3,2,1,0:T(8,128)S(1)}, f32[1,64,64,128]{3,2,1,0:T(8,128)S(1)}, u32[]{:S(2)}, u32[]{:S(2)}) collective-permute-start(f32[1,64,64,128]{3,2,1,0:T(8,128)S(1)} %get-tuple-element.19), channel_id=1, source_target_pairs={{0,8},{8,16},{16,24},{24,32},{32,40},{40,48},{48,56},{56,64},{64,7... | collective-permute-start | bytes 6291464 | tf_op jit(solution)/shard_map/ppermute | solution.py:17
  94.4 47.4 %collective-permute-start.7 = (f32[1,64,64,128]{3,2,1,0:T(8,128)S(1)}, f32[1,64,64,128]{3,2,1,0:T(8,128)}, u32[]{:S(2)}, u32[]{:S(2)}) collective-permute-start(f32[1,64,64,128]{3,2,1,0:T(8,128)S(1)} %get-tuple-element.20), channel_id=1, source_target_pairs={{8,0},{16,8},{24,16},{32,24},{40,32},{48,40},{56,48},{64,56},{72,6... | collective-permute-start | bytes 6291464 | tf_op jit(solution)/shard_map/ppermute | solution.py:18
  96.7 7.6 %collective-permute-start.8 = (f32[4,1,64,128]{3,2,1,0:T(8,128)S(1)}, f32[4,1,64,128]{3,2,1,0:T(8,128)S(1)}, u32[]{:S(2)}, u32[]{:S(2)}) collective-permute-start(f32[4,1,64,128]{3,2,1,0:T(8,128)S(1)} %get-tuple-element.21), channel_id=1, source_target_pairs={{0,2},{2,4},{4,6},{1,3},{3,5},{5,7},{8,10},{10,12},{12,14},{9,11},... | collective-permute-start | bytes 393224 | tf_op jit(solution)/shard_map/ppermute | solution.py:17
  99.9 8.4 %collective-permute-start.9 = (f32[4,1,64,128]{3,2,1,0:T(8,128)S(1)}, f32[4,1,64,128]{3,2,1,0:T(8,128)S(1)}, u32[]{:S(2)}, u32[]{:S(2)}) collective-permute-start(f32[4,1,64,128]{3,2,1,0:T(8,128)S(1)} %get-tuple-element.22), channel_id=1, source_target_pairs={{2,0},{4,2},{6,4},{3,1},{5,3},{7,5},{10,8},{12,10},{14,12},{11,9},... | collective-permute-start | bytes 393224 | tf_op jit(solution)/shard_map/ppermute | solution.py:18
  102.9 5.4 %collective-permute-start.10 = (f32[4,64,1,128]{3,1,2,0:T(8,128)S(1)}, f32[4,64,1,128]{3,1,2,0:T(8,128)S(1)}, u32[]{:S(2)}, u32[]{:S(2)}) collective-permute-start(f32[4,64,1,128]{3,1,2,0:T(8,128)S(1)} %bitcast.32), channel_id=1, source_target_pairs={{0,1},{2,3},{4,5},{6,7},{8,9},{10,11},{12,13},{14,15},{16,17},{18,... | collective-permute-start | bytes 393224 | tf_op jit(solution)/shard_map/ppermute | solution.py:17
  104.3 5.0 %collective-permute-start.11 = (f32[4,64,1,128]{3,1,2,0:T(8,128)S(1)}, f32[4,64,1,128]{3,1,2,0:T(8,128)S(1)}, u32[]{:S(2)}, u32[]{:S(2)}) collective-permute-start(f32[4,64,1,128]{3,1,2,0:T(8,128)S(1)} %bitcast.29), channel_id=1, source_target_pairs={{1,0},{3,2},{5,4},{7,6},{9,8},{11,10},{13,12},{15,14},{17,16},{19,... | collective-permute-start | bytes 393224 | tf_op jit(solution)/shard_map/ppermute | solution.py:18
  172.9 45.3 %collective-permute-start.12 = (f32[1,64,64,128]{3,2,1,0:T(8,128)S(1)}, f32[1,64,64,128]{3,2,1,0:T(8,128)S(1)}, u32[]{:S(2)}, u32[]{:S(2)}) collective-permute-start(f32[1,64,64,128]{3,2,1,0:T(8,128)S(1)} %get-tuple-element.13), channel_id=1, source_target_pairs={{0,8},{8,16},{16,24},{24,32},{32,40},{40,48},{48,56},{56,64},{64,7... | collective-permute-start | bytes 6291464 | tf_op jit(solution)/shard_map/ppermute | solution.py:17
  176.0 48.6 %collective-permute-start.13 = (f32[1,64,64,128]{3,2,1,0:T(8,128)S(1)}, f32[1,64,64,128]{3,2,1,0:T(8,128)}, u32[]{:S(2)}, u32[]{:S(2)}) collective-permute-start(f32[1,64,64,128]{3,2,1,0:T(8,128)S(1)} %get-tuple-element.14), channel_id=1, source_target_pairs={{8,0},{16,8},{24,16},{32,24},{40,32},{48,40},{56,48},{64,56},{72,6... | collective-permute-start | bytes 6291464 | tf_op jit(solution)/shard_map/ppermute | solution.py:18
  178.3 7.6 %collective-permute-start.14 = (f32[4,1,64,128]{3,2,1,0:T(8,128)S(1)}, f32[4,1,64,128]{3,2,1,0:T(8,128)S(1)}, u32[]{:S(2)}, u32[]{:S(2)}) collective-permute-start(f32[4,1,64,128]{3,2,1,0:T(8,128)S(1)} %get-tuple-element.15), channel_id=1, source_target_pairs={{0,2},{2,4},{4,6},{1,3},{3,5},{5,7},{8,10},{10,12},{12,14},{9,11},... | collective-permute-start | bytes 393224 | tf_op jit(solution)/shard_map/ppermute | solution.py:17
  181.5 9.7 %collective-permute-start.15 = (f32[4,1,64,128]{3,2,1,0:T(8,128)S(1)}, f32[4,1,64,128]{3,2,1,0:T(8,128)S(1)}, u32[]{:S(2)}, u32[]{:S(2)}) collective-permute-start(f32[4,1,64,128]{3,2,1,0:T(8,128)S(1)} %get-tuple-element.16), channel_id=1, source_target_pairs={{2,0},{4,2},{6,4},{3,1},{5,3},{7,5},{10,8},{12,10},{14,12},{11,9},... | collective-permute-start | bytes 393224 | tf_op jit(solution)/shard_map/ppermute | solution.py:18
  184.5 6.7 %collective-permute-start.16 = (f32[4,64,1,128]{3,1,2,0:T(8,128)S(1)}, f32[4,64,1,128]{3,1,2,0:T(8,128)S(1)}, u32[]{:S(2)}, u32[]{:S(2)}) collective-permute-start(f32[4,64,1,128]{3,1,2,0:T(8,128)S(1)} %bitcast.33), channel_id=1, source_target_pairs={{0,1},{2,3},{4,5},{6,7},{8,9},{10,11},{12,13},{14,15},{16,17},{18,... | collective-permute-start | bytes 393224 | tf_op jit(solution)/shard_map/ppermute | solution.py:17
  185.8 6.1 %collective-permute-start.17 = (f32[4,64,1,128]{3,1,2,0:T(8,128)S(1)}, f32[4,64,1,128]{3,1,2,0:T(8,128)S(1)}, u32[]{:S(2)}, u32[]{:S(2)}) collective-permute-start(f32[4,64,1,128]{3,1,2,0:T(8,128)S(1)} %bitcast.30), channel_id=1, source_target_pairs={{1,0},{3,2},{5,4},{7,6},{9,8},{11,10},{13,12},{15,14},{17,16},{19,... | collective-permute-start | bytes 393224 | tf_op jit(solution)/shard_map/ppermute | solution.py:18
  255.6 46.4 %collective-permute-start.18 = (f32[1,64,64,128]{3,2,1,0:T(8,128)S(1)}, f32[1,64,64,128]{3,2,1,0:T(8,128)S(1)}, u32[]{:S(2)}, u32[]{:S(2)}) collective-permute-start(f32[1,64,64,128]{3,2,1,0:T(8,128)S(1)} %get-tuple-element.7), channel_id=1, source_target_pairs={{0,8},{8,16},{16,24},{24,32},{32,40},{40,48},{48,56},{56,64},{64,7... | collective-permute-start | bytes 6291464 | tf_op jit(solution)/shard_map/ppermute | solution.py:17
  260.7 45.4 %collective-permute-start.19 = (f32[1,64,64,128]{3,2,1,0:T(8,128)S(1)}, f32[1,64,64,128]{3,2,1,0:T(8,128)}, u32[]{:S(2)}, u32[]{:S(2)}) collective-permute-start(f32[1,64,64,128]{3,2,1,0:T(8,128)S(1)} %get-tuple-element.8), channel_id=1, source_target_pairs={{8,0},{16,8},{24,16},{32,24},{40,32},{48,40},{56,48},{64,56},{72,6... | collective-permute-start | bytes 6291464 | tf_op jit(solution)/shard_map/ppermute | solution.py:18
  263.0 12.3 %collective-permute-start.20 = (f32[4,1,64,128]{3,2,1,0:T(8,128)S(1)}, f32[4,1,64,128]{3,2,1,0:T(8,128)S(1)}, u32[]{:S(2)}, u32[]{:S(2)}) collective-permute-start(f32[4,1,64,128]{3,2,1,0:T(8,128)S(1)} %get-tuple-element.9), channel_id=1, source_target_pairs={{0,2},{2,4},{4,6},{1,3},{3,5},{5,7},{8,10},{10,12},{12,14},{9,11},... | collective-permute-start | bytes 393224 | tf_op jit(solution)/shard_map/ppermute | solution.py:17
  266.2 10.4 %collective-permute-start.21 = (f32[4,1,64,128]{3,2,1,0:T(8,128)S(1)}, f32[4,1,64,128]{3,2,1,0:T(8,128)S(1)}, u32[]{:S(2)}, u32[]{:S(2)}) collective-permute-start(f32[4,1,64,128]{3,2,1,0:T(8,128)S(1)} %get-tuple-element.10), channel_id=1, source_target_pairs={{2,0},{4,2},{6,4},{3,1},{5,3},{7,5},{10,8},{12,10},{14,12},{11,9},... | collective-permute-start | bytes 393224 | tf_op jit(solution)/shard_map/ppermute | solution.py:18
  269.2 7.4 %collective-permute-start.23 = (f32[4,64,1,128]{3,1,2,0:T(8,128)S(1)}, f32[4,64,1,128]{3,1,2,0:T(8,128)S(1)}, u32[]{:S(2)}, u32[]{:S(2)}) collective-permute-start(f32[4,64,1,128]{3,1,2,0:T(8,128)S(1)} %bitcast.31), channel_id=1, source_target_pairs={{1,0},{3,2},{5,4},{7,6},{9,8},{11,10},{13,12},{15,14},{17,16},{19,... | collective-permute-start | bytes 393224 | tf_op jit(solution)/shard_map/ppermute | solution.py:18
  275.2 3.2 collective-permute-start.22
where the time goes:
time: 341 us; the launch traced here: 335 us
  waiting for transfers between devices  130 us (38%)
  other arithmetic  112 us (33%)
  starting transfers between devices  63.4 us (19%)
  local copies, waits for them, and re-layouts  29.2 us (9%)
    ppermute x12, waiting for transfers between devices, with_halo(): lax.ppermute(last, axis, up)  114 us
    add x4, other arithmetic, advance(): return 2.0 * middle - before + speed_square * spread  112 us
    ppermute x12, starting transfers between devices, with_halo(): lax.ppermute(last, axis, up)  34.6 us
    ppermute x12, starting transfers between devices, with_halo(): lax.ppermute(leading, axis, [(b, a) for a, b in up])  28.8 us
    ppermute x12, waiting for transfers between devices, with_halo(): lax.ppermute(leading, axis, [(b, a) for a, b in up])  16.2 us
    slice x11, local copies, waits for them, and re-layouts, with_halo(): last = lax.slice_in_dim(array, length - width, length, axis=dim)  16 us
    unnamed x10, local copies, waits for them, and re-layouts  7.47 us
  transfers between devices with their start and end apart: 24, of which 10 were waited for; matrix products, arithmetic and copies ran while one was open for 5% of the time, Pallas kernels for 0%

commit v1 on v0

v1 whole, which is shorter than its diff:
```python
import jax
import jax.numpy as jnp
from jax import lax
from jax.experimental import pallas as pl
from jax.experimental.pallas import tpu as pltpu
from jax.sharding import PartitionSpec as P

STEPS = 4
CHUNKS = 8
MESH = pl.DeviceIdType.MESH


def kernel(
    p_in, e_in, c_in, out, even, odd, c, z_out, z_in,
    load_sem, y_send, y_recv, x_send, x_recv, z_send, z_recv,
):
    planes, rows, depth, levels = p_in.shape
    size = rows // CHUNKS
    lat, lon, lev = (lax.axis_index(name) for name in ("lat", "lon", "lev"))
    field = (even, odd)
    y_has = (lat > 0, lat < lax.axis_size("lat") - 1)
    x_has = (lon > 0, lon < lax.axis_size("lon") - 1)
    y_to = ({"lat": lat - 1}, {"lat": lat + 1})
    x_to = ({"lon": lon - 1}, {"lon": lon + 1})
    z_to = {"lev": 1 - lev}

    def y_rows(chunk, pad):
        return pl.ds(pad + chunk * size, size)

    def y_start(t, side, chunk):
        if t == 0:
            source = p_in.at[(0, planes - 1)[side], y_rows(chunk, 0)]
        else:
            source = field[t % 2].at[(1, planes)[side], y_rows(chunk, 1)]
        return pltpu.make_async_remote_copy(
            src_ref=source,
            dst_ref=field[t % 2].at[(planes + 1, 0)[side], y_rows(chunk, 1)],
            send_sem=y_send.at[t, side, chunk],
            recv_sem=y_recv.at[t, 1 - side, chunk],
            device_id=y_to[side],
            device_id_type=MESH,
        )

    def y_arrival(t, side, chunk):
        halo = field[t % 2].at[(0, planes + 1)[side], y_rows(chunk, 1)]
        return pltpu.make_async_remote_copy(
            src_ref=halo,
            dst_ref=halo,
            send_sem=y_send.at[t, side, chunk],
            recv_sem=y_recv.at[t, side, chunk],
            device_id=y_to[side],
            device_id_type=MESH,
        )

    def x_start(t, side):
        if t == 0:
            source = p_in.at[:, (0, rows - 1)[side]]
        else:
            source = field[t % 2].at[pl.ds(1, planes), (1, rows)[side]]
        return pltpu.make_async_remote_copy(
            src_ref=source,
            dst_ref=field[t % 2].at[pl.ds(1, planes), (rows + 1, 0)[side]],
            send_sem=x_send.at[t, side],
            recv_sem=x_recv.at[t, 1 - side],
            device_id=x_to[side],
            device_id_type=MESH,
        )

    def x_arrival(t, side):
        halo = field[t % 2].at[pl.ds(1, planes), (0, rows + 1)[side]]
        return pltpu.make_async_remote_copy(
            src_ref=halo,
            dst_ref=halo,
            send_sem=x_send.at[t, side],
            recv_sem=x_recv.at[t, side],
            device_id=x_to[side],
            device_id_type=MESH,
        )

    def z_copy(t):
        return pltpu.make_async_remote_copy(
            src_ref=z_out.at[t],
            dst_ref=z_in.at[t],
            send_sem=z_send.at[t],
            recv_sem=z_recv.at[t],
            device_id=z_to,
            device_id_type=MESH,
        )

    def on_sides(has, action):
        for side in (0, 1):
            pl.when(has[side])(lambda side=side: action(side))

    inner = (pl.ds(1, planes), pl.ds(1, rows))
    loads = [
        pltpu.make_async_copy(p_in, even.at[inner], load_sem.at[0]),
        pltpu.make_async_copy(e_in, odd.at[inner], load_sem.at[1]),
        pltpu.make_async_copy(c_in, c, load_sem.at[2]),
    ]
    for load in loads:
        load.start()
    barrier = pltpu.get_barrier_semaphore()

    def greet(device):
        pl.semaphore_signal(barrier, inc=1, device_id=device, device_id_type=MESH)

    greet(z_to)
    on_sides(y_has, lambda side: greet(y_to[side]))
    on_sides(x_has, lambda side: greet(x_to[side]))
    peers = 1 + sum(jnp.where(has, 1, 0) for has in y_has + x_has)
    pl.semaphore_wait(barrier, peers)

    def first_sends(chunk, carry):
        on_sides(y_has, lambda side: y_start(0, side, chunk).start())
        return carry

    lax.fori_loop(0, CHUNKS, first_sends, 0)
    on_sides(x_has, lambda side: x_start(0, side).start())

    nothing = jnp.zeros((depth, levels), jnp.float32)

    def clear_plane(side):
        @pl.when(jnp.logical_not(y_has[side]))
        def _():
            def one(row, carry):
                for ref in field:
                    ref[(0, planes + 1)[side], row + 1] = nothing
                return carry

            lax.fori_loop(0, rows, one, 0)

    def clear_row(side):
        @pl.when(jnp.logical_not(x_has[side]))
        def _():
            for ref in field:
                for plane in range(planes):
                    ref[plane + 1, (0, rows + 1)[side]] = nothing

    for side in (0, 1):
        clear_plane(side)
        clear_row(side)

    below, above = (lev == 1), (lev == 0)
    place = lax.broadcasted_iota(jnp.int32, (depth, levels), 0)

    def keep_face(t, plane, row, values):
        face = jnp.where(above, values[depth - 1 :], values[:1])
        z_out[t, plane, pl.ds(row, 1)] = face

    def advance(t, plane, row):
        now, other = field[t % 2], field[1 - t % 2]
        middle = now[plane + 1, row + 1]
        beside = z_in[t, plane, pl.ds(row, 1)]
        lower = jnp.where(place == 0, jnp.where(below, beside, 0.0), pltpu.roll(middle, 1, 0))
        upper = jnp.where(
            place == depth - 1, jnp.where(above, beside, 0.0), pltpu.roll(middle, depth - 1, 0)
        )
        total = now[plane, row + 1] + now[plane + 2, row + 1]
        total = total + now[plane + 1, row] + now[plane + 1, row + 2] + lower + upper
        spread = total - 6.0 * middle
        later = 2.0 * middle - other[plane + 1, row + 1] + c[plane, row] * spread
        if t < STEPS - 1:
            other[plane + 1, row + 1] = later
            keep_face(t + 1, plane, row, later)
        else:
            out[plane, row] = later

    for load in loads:
        load.wait()

    def first_face(row, carry):
        for plane in range(planes):
            keep_face(0, plane, row, even[plane + 1, row + 1])
        return carry

    lax.fori_loop(0, rows, first_face, 0)
    z_copy(0).start()

    for t in range(STEPS):
        if t > 0:
            on_sides(x_has, lambda side: x_start(t - 1, side).wait_send())
        on_sides(x_has, lambda side: x_arrival(t, side).wait_recv())
        z_copy(t).wait_recv()

        def inside(row, carry):
            for plane in range(1, planes - 1):
                advance(t, plane, row)
            return carry

        lax.fori_loop(0, rows, inside, 0)

        def outside(chunk, carry):
            if t > 0:
                on_sides(y_has, lambda side: y_start(t - 1, side, chunk).wait_send())
            on_sides(y_has, lambda side: y_arrival(t, side, chunk).wait_recv())

            def one(row, carry):
                for plane in (0, planes - 1):
                    advance(t, plane, chunk * size + row)
                return carry

            lax.fori_loop(0, size, one, 0)
            if t < STEPS - 1:
                on_sides(y_has, lambda side: y_start(t + 1, side, chunk).start())
            return carry

        lax.fori_loop(0, CHUNKS, outside, 0)
        if t < STEPS - 1:
            on_sides(x_has, lambda side: x_start(t + 1, side).start())
            z_copy(t + 1).start()

    last = STEPS - 1

    def last_sends(chunk, carry):
        on_sides(y_has, lambda side: y_start(last, side, chunk).wait_send())
        return carry

    lax.fori_loop(0, CHUNKS, last_sends, 0)
    on_sides(x_has, lambda side: x_start(last, side).wait_send())
    for t in range(STEPS):
        z_copy(t).wait_send()


def shards(pressure, earlier, speed_square):
    planes, rows, depth, levels = pressure.shape
    padded = (planes + 2, rows + 2, depth, levels)
    return pl.pallas_call(
        kernel,
        out_shape=pltpu.VMEM(pressure.shape, jnp.float32),
        in_specs=[pl.BlockSpec(memory_space=pltpu.HBM)] * 3,
        out_specs=pl.BlockSpec(memory_space=pltpu.VMEM),
        scratch_shapes=[
            pltpu.VMEM(padded, jnp.float32),
            pltpu.VMEM(padded, jnp.float32),
            pltpu.VMEM(pressure.shape, jnp.float32),
            pltpu.VMEM((STEPS, planes, rows, levels), jnp.float32),
            pltpu.VMEM((STEPS, planes, rows, levels), jnp.float32),
            pltpu.SemaphoreType.DMA((3,)),
            pltpu.SemaphoreType.DMA((STEPS, 2, CHUNKS)),
            pltpu.SemaphoreType.DMA((STEPS, 2, CHUNKS)),
            pltpu.SemaphoreType.DMA((STEPS, 2)),
            pltpu.SemaphoreType.DMA((STEPS, 2)),
            pltpu.SemaphoreType.DMA((STEPS,)),
            pltpu.SemaphoreType.DMA((STEPS,)),
        ],
        compiler_params=pltpu.CompilerParams(
            collective_id=0, has_side_effects=True, vmem_limit_bytes=48 * 2**20
        ),
    )(pressure, earlier, speed_square)


def solution(mesh):
    spec = P("lat", "lon", "lev", None)
    return jax.shard_map(
        shards, mesh=mesh, in_specs=(spec,) * 3, out_specs=spec, check_vma=False
    )
```

time: 341 us -> 190 us (0.56); the launches traced: 335 us -> 189 us
  Pallas kernels: 0 us -> 185 us
  waiting for transfers between devices: 130 us -> 0 us
  other arithmetic: 112 us -> 0 us
  starting transfers between devices: 63.4 us -> 0 us
  local copies, waits for them, and re-layouts: 29.2 us -> 3.4 us
    pallas_call x0 -> x1, Pallas kernels: none -> 185 us  [shards(): pl.pallas_call(kernel, out_shape=pltpu.VMEM(pressure.shape, jnp.float32),...]
    ppermute x24 -> x0, waiting for transfers between devices: 130 us -> none  [the longest x12 114 us: with_halo(): lax.ppermute(last, axis, up)]
    add x4 -> x0, other arithmetic: 112 us -> none  [advance(): return 2.0 * middle - before + speed_square * spread]
    ppermute x24 -> x0, starting transfers between devices: 63.4 us -> none  [the longest x12 34.6 us: with_halo(): lax.ppermute(last, axis, up)]
    slice x12 -> x0, local copies, waits for them, and re-layouts: 20.1 us -> none  [the longest x11 16 us: with_halo(): last = lax.slice_in_dim(array, length - width, length, axis=dim)]
    unnamed x10 -> x1, local copies, waits for them, and re-layouts: 7.47 us -> 3.4 us
  transfers between devices with their start and end apart: 24 -> 0, of which waited for: 10 -> 0; matrix products, arithmetic and copies ran while one was open for 5% -> 0% of each run, Pallas kernels for 0% -> 0%
where the time goes in v1:
time: 190 us; the launch traced here: 189 us
  Pallas kernels  185 us (97%)
  local copies, waits for them, and re-layouts  3.4 us (2%)
    pallas_call x1, Pallas kernels, shards(): pl.pallas_call(kernel, out_shape=pltpu.VMEM(pressure.shape, jnp.float32),...  185 us

profile of v1, /device:TPU:1, one launch (start us, length us, event | category | flops | bytes accessed | tf_op | source)
XLA Modules:
  0.0 188.6 jit_solution(7053796748771834277)
XLA Ops:
  0.0 185.2 %shard_map.37 = f32[4,64,64,128]{3,2,1,0:T(8,128)S(1)} custom-call(f32[4,64,64,128]{3,2,1,0:T(8,128)} %p_in.1, f32[4,64,64,128]{3,2,1,0:T(8,128)} %e_in.1, f32[4,64,64,128]{3,2,1,0:T(8,128)} %c_in.1), custom_call_target="tpu_custom_call" | custom-call | tf_op jit(solution)/shard_map/pallas_call | solution.py:227
  185.2 3.4 %copy.5 = f32[4,64,64,128]{3,2,1,0:T(8,128)} copy(f32[4,64,64,128]{3,2,1,0:T(8,128)S(1)} %shard_map.37) | data formatting | bytes 16777216

commit v2 on v1

--- a/solution.py
+++ b/solution.py
@@ -24,17 +24,13 @@
     x_to = ({"lon": lon - 1}, {"lon": lon + 1})
     z_to = {"lev": 1 - lev}
 
-    def y_rows(chunk, pad):
-        return pl.ds(pad + chunk * size, size)
+    def y_rows(chunk):
+        return pl.ds(1 + chunk * size, size)
 
     def y_start(t, side, chunk):
-        if t == 0:
-            source = p_in.at[(0, planes - 1)[side], y_rows(chunk, 0)]
-        else:
-            source = field[t % 2].at[(1, planes)[side], y_rows(chunk, 1)]
-        return pltpu.make_async_remote_copy(
-            src_ref=source,
-            dst_ref=field[t % 2].at[(planes + 1, 0)[side], y_rows(chunk, 1)],
+        return pltpu.make_async_remote_copy(
+            src_ref=field[t % 2].at[(1, planes)[side], y_rows(chunk)],
+            dst_ref=field[t % 2].at[(planes + 1, 0)[side], y_rows(chunk)],
             send_sem=y_send.at[t, side, chunk],
             recv_sem=y_recv.at[t, 1 - side, chunk],
             device_id=y_to[side],
@@ -42,7 +38,7 @@
         )
 
     def y_arrival(t, side, chunk):
-        halo = field[t % 2].at[(0, planes + 1)[side], y_rows(chunk, 1)]
+        halo = field[t % 2].at[(0, planes + 1)[side], y_rows(chunk)]
         return pltpu.make_async_remote_copy(
             src_ref=halo,
             dst_ref=halo,
@@ -91,30 +87,48 @@
         for side in (0, 1):
             pl.when(has[side])(lambda side=side: action(side))
 
-    inner = (pl.ds(1, planes), pl.ds(1, rows))
-    loads = [
-        pltpu.make_async_copy(p_in, even.at[inner], load_sem.at[0]),
-        pltpu.make_async_copy(e_in, odd.at[inner], load_sem.at[1]),
-        pltpu.make_async_copy(c_in, c, load_sem.at[2]),
-    ]
-    for load in loads:
-        load.start()
     barrier = pltpu.get_barrier_semaphore()
 
     def greet(device):
         pl.semaphore_signal(barrier, inc=1, device_id=device, device_id_type=MESH)
 
-    greet(z_to)
     on_sides(y_has, lambda side: greet(y_to[side]))
     on_sides(x_has, lambda side: greet(x_to[side]))
+    greet(z_to)
+
+    def load_pressure(number, first, count, start, length):
+        return pltpu.make_async_copy(
+            p_in.at[pl.ds(first, count), pl.ds(start, length)],
+            even.at[pl.ds(first + 1, count), pl.ds(start + 1, length)],
+            load_sem.at[number],
+        )
+
+    heads = [load_pressure(side, (0, planes - 1)[side], 1, 0, size) for side in (0, 1)]
+    tails = [
+        load_pressure(2 + side, (0, planes - 1)[side], 1, size, rows - size) for side in (0, 1)
+    ]
+    loads = [
+        load_pressure(4, 1, planes - 2, 0, rows),
+        pltpu.make_async_copy(
+            e_in, odd.at[pl.ds(1, planes), pl.ds(1, rows)], load_sem.at[5]
+        ),
+        pltpu.make_async_copy(c_in, c, load_sem.at[6]),
+    ]
+    for load in heads + tails + loads:
+        load.start()
     peers = 1 + sum(jnp.where(has, 1, 0) for has in y_has + x_has)
     pl.semaphore_wait(barrier, peers)
+    for load in heads:
+        load.wait()
+    on_sides(y_has, lambda side: y_start(0, side, 0).start())
+    for load in tails:
+        load.wait()
 
     def first_sends(chunk, carry):
         on_sides(y_has, lambda side: y_start(0, side, chunk).start())
         return carry
 
-    lax.fori_loop(0, CHUNKS, first_sends, 0)
+    lax.fori_loop(1, CHUNKS, first_sends, 0)
     on_sides(x_has, lambda side: x_start(0, side).start())
 
     nothing = jnp.zeros((depth, levels), jnp.float32)
@@ -149,21 +163,25 @@
 
     def advance(t, plane, row):
         now, other = field[t % 2], field[1 - t % 2]
+        last = t == STEPS - 1
         middle = now[plane + 1, row + 1]
         beside = z_in[t, plane, pl.ds(row, 1)]
         lower = jnp.where(place == 0, jnp.where(below, beside, 0.0), pltpu.roll(middle, 1, 0))
         upper = jnp.where(
             place == depth - 1, jnp.where(above, beside, 0.0), pltpu.roll(middle, depth - 1, 0)
         )
-        total = now[plane, row + 1] + now[plane + 2, row + 1]
-        total = total + now[plane + 1, row] + now[plane + 1, row + 2] + lower + upper
+        total = now[plane + 1, row] + now[plane + 1, row + 2] + lower + upper
+        if not (last and plane == 0):
+            total = total + now[plane, row + 1]
+        if not (last and plane == planes - 1):
+            total = total + now[plane + 2, row + 1]
         spread = total - 6.0 * middle
         later = 2.0 * middle - other[plane + 1, row + 1] + c[plane, row] * spread
-        if t < STEPS - 1:
+        if last:
+            out[plane, row] = later
+        else:
             other[plane + 1, row + 1] = later
             keep_face(t + 1, plane, row, later)
-        else:
-            out[plane, row] = later
 
     for load in loads:
         load.wait()
@@ -177,17 +195,20 @@
     z_copy(0).start()
 
     for t in range(STEPS):
+        last = t == STEPS - 1
         if t > 0:
             on_sides(x_has, lambda side: x_start(t - 1, side).wait_send())
         on_sides(x_has, lambda side: x_arrival(t, side).wait_recv())
         z_copy(t).wait_recv()
 
         def inside(row, carry):
-            for plane in range(1, planes - 1):
+            for plane in range(planes) if last else range(1, planes - 1):
                 advance(t, plane, row)
             return carry
 
         lax.fori_loop(0, rows, inside, 0)
+        if last:
+            break
 
         def outside(chunk, carry):
             if t > 0:
@@ -200,25 +221,33 @@
                 return carry
 
             lax.fori_loop(0, size, one, 0)
-            if t < STEPS - 1:
-                on_sides(y_has, lambda side: y_start(t + 1, side, chunk).start())
+            on_sides(y_has, lambda side: y_start(t + 1, side, chunk).start())
             return carry
 
         lax.fori_loop(0, CHUNKS, outside, 0)
-        if t < STEPS - 1:
-            on_sides(x_has, lambda side: x_start(t + 1, side).start())
-            z_copy(t + 1).start()
-
-    last = STEPS - 1
-
-    def last_sends(chunk, carry):
-        on_sides(y_has, lambda side: y_start(last, side, chunk).wait_send())
+        on_sides(x_has, lambda side: x_start(t + 1, side).start())
+        z_copy(t + 1).start()
+
+    t = STEPS - 1
+    on_sides(x_has, lambda side: x_start(t, side).wait_send())
+    for step in range(STEPS):
+        z_copy(step).wait_send()
+
+    def closing(chunk, carry):
+        on_sides(y_has, lambda side: y_start(t - 1, side, chunk).wait_send())
+
+        def add(side):
+            y_arrival(t, side, chunk).wait_recv()
+            plane = (0, planes - 1)[side]
+            here = pl.ds(chunk * size, size)
+            halo = field[t % 2][(0, planes + 1)[side], y_rows(chunk)]
+            out[plane, here] = out[plane, here] + c[plane, here] * halo
+
+        on_sides(y_has, add)
+        on_sides(y_has, lambda side: y_start(t, side, chunk).wait_send())
         return carry
 
-    lax.fori_loop(0, CHUNKS, last_sends, 0)
-    on_sides(x_has, lambda side: x_start(last, side).wait_send())
-    for t in range(STEPS):
-        z_copy(t).wait_send()
+    lax.fori_loop(0, CHUNKS, closing, 0)
 
 
 def shards(pressure, earlier, speed_square):
@@ -235,7 +264,7 @@
             pltpu.VMEM(pressure.shape, jnp.float32),
             pltpu.VMEM((STEPS, planes, rows, levels), jnp.float32),
             pltpu.VMEM((STEPS, planes, rows, levels), jnp.float32),
-            pltpu.SemaphoreType.DMA((3,)),
+            pltpu.SemaphoreType.DMA((7,)),
             pltpu.SemaphoreType.DMA((STEPS, 2, CHUNKS)),
             pltpu.SemaphoreType.DMA((STEPS, 2, CHUNKS)),
             pltpu.SemaphoreType.DMA((STEPS, 2)),

time: 190 us -> 189 us (level)
  no operation moved by 1% of the time
where the time goes in v2:
time: 189 us; the launch traced here: 188 us
  Pallas kernels  185 us (98%)
  local copies, waits for them, and re-layouts  3.4 us (2%)
    pallas_call x1, Pallas kernels, shards(): pl.pallas_call(kernel, out_shape=pltpu.VMEM(pressure.shape, jnp.float32),...  185 us

profile of v2, /device:TPU:1, one launch (start us, length us, event | category | flops | bytes accessed | tf_op | source)
XLA Modules:
  0.0 188.1 jit_solution(9506219874003403232)
XLA Ops:
  0.0 184.7 %shard_map.37 = f32[4,64,64,128]{3,2,1,0:T(8,128)S(1)} custom-call(f32[4,64,64,128]{3,2,1,0:T(8,128)} %p_in.1, f32[4,64,64,128]{3,2,1,0:T(8,128)} %e_in.1, f32[4,64,64,128]{3,2,1,0:T(8,128)} %c_in.1), custom_call_target="tpu_custom_call" | custom-call | tf_op jit(solution)/shard_map/pallas_call | solution.py:256
  184.7 3.4 %copy.5 = f32[4,64,64,128]{3,2,1,0:T(8,128)} copy(f32[4,64,64,128]{3,2,1,0:T(8,128)S(1)} %shard_map.37) | data formatting | bytes 16777216

commit v3 on v2

--- a/solution.py
+++ b/solution.py
@@ -6,16 +6,18 @@
 from jax.sharding import PartitionSpec as P
 
 STEPS = 4
-CHUNKS = 8
+CUTS = (0, 28, 56, 64)
+CHUNKS = len(CUTS) - 1
+RING = 4
+RELIEF = 2
 MESH = pl.DeviceIdType.MESH
 
 
 def kernel(
     p_in, e_in, c_in, out, even, odd, c, z_out, z_in,
-    load_sem, y_send, y_recv, x_send, x_recv, z_send, z_recv,
+    passed, load_sem, y_send, y_recv, x_send, x_recv, z_send, z_recv, hop_sem,
 ):
     planes, rows, depth, levels = p_in.shape
-    size = rows // CHUNKS
     lat, lon, lev = (lax.axis_index(name) for name in ("lat", "lon", "lev"))
     field = (even, odd)
     y_has = (lat > 0, lat < lax.axis_size("lat") - 1)
@@ -24,21 +26,51 @@
     x_to = ({"lon": lon - 1}, {"lon": lon + 1})
     z_to = {"lev": 1 - lev}
 
-    def y_rows(chunk):
-        return pl.ds(1 + chunk * size, size)
-
-    def y_start(t, side, chunk):
-        return pltpu.make_async_remote_copy(
-            src_ref=field[t % 2].at[(1, planes)[side], y_rows(chunk)],
-            dst_ref=field[t % 2].at[(planes + 1, 0)[side], y_rows(chunk)],
+    rings = lax.axis_size("lat") // RING
+    detours = []
+    for q in range(rings - 1):
+        end, start = q * RING + RING - 1, q * RING + RING
+        detours.append((1, end, end + RING, start, RELIEF * (q + 1)))
+        detours.append((0, start, start - RING, end, RELIEF * (rings - 1 - q)))
+    ring_place = lax.rem(lat, RING)
+    at_start, at_end = (ring_place == 0), (ring_place == RING - 1)
+    wraps = (at_start, at_end)
+
+    def hop(side, relay, count):
+        return pltpu.make_async_remote_copy(
+            src_ref=field[0].at[(1, planes)[side], pl.ds(1 + rows - count, count)],
+            dst_ref=passed.at[pl.ds(0, count)],
+            send_sem=hop_sem.at[0],
+            recv_sem=hop_sem.at[1],
+            device_id={"lat": relay},
+            device_id_type=MESH,
+        )
+
+    def forward(side, dest, count):
+        return pltpu.make_async_remote_copy(
+            src_ref=passed.at[pl.ds(0, count)],
+            dst_ref=field[0].at[(planes + 1, 0)[side], pl.ds(1 + rows - count, count)],
+            send_sem=hop_sem.at[2],
+            recv_sem=hop_sem.at[3],
+            device_id={"lat": dest},
+            device_id_type=MESH,
+        )
+
+    def y_rows(chunk, less=0):
+        return pl.ds(1 + CUTS[chunk], CUTS[chunk + 1] - CUTS[chunk] - less)
+
+    def y_start(t, side, chunk, less=0):
+        return pltpu.make_async_remote_copy(
+            src_ref=field[t % 2].at[(1, planes)[side], y_rows(chunk, less)],
+            dst_ref=field[t % 2].at[(planes + 1, 0)[side], y_rows(chunk, less)],
             send_sem=y_send.at[t, side, chunk],
             recv_sem=y_recv.at[t, 1 - side, chunk],
             device_id=y_to[side],
             device_id_type=MESH,
         )
 
-    def y_arrival(t, side, chunk):
-        halo = field[t % 2].at[(0, planes + 1)[side], y_rows(chunk)]
+    def y_arrival(t, side, chunk, less=0):
+        halo = field[t % 2].at[(0, planes + 1)[side], y_rows(chunk, less)]
         return pltpu.make_async_remote_copy(
             src_ref=halo,
             dst_ref=halo,
@@ -48,6 +80,34 @@
             device_id_type=MESH,
         )
 
+    def sending(t, chunk, action):
+        detoured = t == 0 and chunk == CHUNKS - 1
+        for side in (0, 1):
+            direct = y_has[side]
+            if detoured:
+                direct = direct & jnp.logical_not(wraps[side])
+            pl.when(direct)(lambda side=side: action(y_start(t, side, chunk)))
+        for side, origin, relay, dest, count in detours if detoured else ():
+
+            @pl.when(lat == origin)
+            def _():
+                action(y_start(t, side, chunk, count))
+                action(hop(side, relay, count))
+
+    def arriving(t, side, chunk):
+        detoured = t == 0 and chunk == CHUNKS - 1
+        direct = y_has[side]
+        if detoured:
+            direct = direct & jnp.logical_not(wraps[side])
+        pl.when(direct)(lambda: y_arrival(t, side, chunk).wait_recv())
+        for way, origin, relay, dest, count in detours if detoured else ():
+            if way != side:
+
+                @pl.when(lat == dest)
+                def _():
+                    y_arrival(t, side, chunk, count).wait_recv()
+                    forward(way, dest, count).wait_recv()
+
     def x_start(t, side):
         if t == 0:
             source = p_in.at[:, (0, rows - 1)[side]]
@@ -95,6 +155,11 @@
     on_sides(y_has, lambda side: greet(y_to[side]))
     on_sides(x_has, lambda side: greet(x_to[side]))
     greet(z_to)
+    outer = at_start | at_end
+    ring_has = (outer & (lat >= RING), outer & (lat < (rings - 1) * RING))
+    if rings > 1:
+        on_sides(ring_has, lambda side: greet({"lat": lat + (-RING, RING)[side]}))
+        on_sides(wraps, lambda side: greet({"lat": lat + (RING - 1, 1 - RING)[side]}))
 
     def load_pressure(number, first, count, start, length):
         return pltpu.make_async_copy(
@@ -103,9 +168,10 @@
             load_sem.at[number],
         )
 
-    heads = [load_pressure(side, (0, planes - 1)[side], 1, 0, size) for side in (0, 1)]
+    ends = (0, planes - 1)
+    heads = [load_pressure(side, ends[side], 1, 0, CUTS[1]) for side in (0, 1)]
     tails = [
-        load_pressure(2 + side, (0, planes - 1)[side], 1, size, rows - size) for side in (0, 1)
+        load_pressure(2 + side, ends[side], 1, CUTS[1], rows - CUTS[1]) for side in (0, 1)
     ]
     loads = [
         load_pressure(4, 1, planes - 2, 0, rows),
@@ -116,19 +182,17 @@
     ]
     for load in heads + tails + loads:
         load.start()
-    peers = 1 + sum(jnp.where(has, 1, 0) for has in y_has + x_has)
+    others = y_has + x_has + (ring_has + wraps if rings > 1 else ())
+    peers = 1 + sum(jnp.where(has, 1, 0) for has in others)
     pl.semaphore_wait(barrier, peers)
     for load in heads:
         load.wait()
-    on_sides(y_has, lambda side: y_start(0, side, 0).start())
+    sending(0, 0, lambda copy: copy.start())
     for load in tails:
         load.wait()
 
-    def first_sends(chunk, carry):
-        on_sides(y_has, lambda side: y_start(0, side, chunk).start())
-        return carry
-
-    lax.fori_loop(1, CHUNKS, first_sends, 0)
+    for chunk in range(1, CHUNKS):
+        sending(0, chunk, lambda copy: copy.start())
     on_sides(x_has, lambda side: x_start(0, side).start())
 
     nothing = jnp.zeros((depth, levels), jnp.float32)
@@ -193,6 +257,13 @@
 
     lax.fori_loop(0, rows, first_face, 0)
     z_copy(0).start()
+    for way, origin, relay, dest, count in detours:
+
+        @pl.when(lat == relay)
+        def _():
+            hop(way, relay, count).wait_recv()
+            forward(way, dest, count).start()
+
 
     for t in range(STEPS):
         last = t == STEPS - 1
@@ -210,44 +281,46 @@
         if last:
             break
 
-        def outside(chunk, carry):
+        for chunk in range(CHUNKS):
             if t > 0:
-                on_sides(y_has, lambda side: y_start(t - 1, side, chunk).wait_send())
-            on_sides(y_has, lambda side: y_arrival(t, side, chunk).wait_recv())
+                sending(t - 1, chunk, lambda copy: copy.wait_send())
+            for side in (0, 1):
+                arriving(t, side, chunk)
 
             def one(row, carry):
                 for plane in (0, planes - 1):
-                    advance(t, plane, chunk * size + row)
+                    advance(t, plane, row)
                 return carry
 
-            lax.fori_loop(0, size, one, 0)
-            on_sides(y_has, lambda side: y_start(t + 1, side, chunk).start())
-            return carry
-
-        lax.fori_loop(0, CHUNKS, outside, 0)
+            lax.fori_loop(CUTS[chunk], CUTS[chunk + 1], one, 0)
+            sending(t + 1, chunk, lambda copy: copy.start())
+
         on_sides(x_has, lambda side: x_start(t + 1, side).start())
         z_copy(t + 1).start()
 
+    for way, origin, relay, dest, count in detours:
+        pl.when(lat == relay)(lambda: forward(way, dest, count).wait_send())
     t = STEPS - 1
     on_sides(x_has, lambda side: x_start(t, side).wait_send())
     for step in range(STEPS):
         z_copy(step).wait_send()
 
-    def closing(chunk, carry):
-        on_sides(y_has, lambda side: y_start(t - 1, side, chunk).wait_send())
+    for chunk in range(CHUNKS):
+        sending(t - 1, chunk, lambda copy: copy.wait_send())
 
         def add(side):
             y_arrival(t, side, chunk).wait_recv()
             plane = (0, planes - 1)[side]
-            here = pl.ds(chunk * size, size)
-            halo = field[t % 2][(0, planes + 1)[side], y_rows(chunk)]
-            out[plane, here] = out[plane, here] + c[plane, here] * halo
+
+            def one(row, carry):
+                halo = field[t % 2][(0, planes + 1)[side], row + 1]
+                out[plane, row] = out[plane, row] + c[plane, row] * halo
+                return carry
+
+            lax.fori_loop(CUTS[chunk], CUTS[chunk + 1], one, 0, unroll=4)
 
         on_sides(y_has, add)
-        on_sides(y_has, lambda side: y_start(t, side, chunk).wait_send())
-        return carry
-
-    lax.fori_loop(0, CHUNKS, closing, 0)
+        sending(t, chunk, lambda copy: copy.wait_send())
 
 
 def shards(pressure, earlier, speed_square):
@@ -264,6 +337,7 @@
             pltpu.VMEM(pressure.shape, jnp.float32),
             pltpu.VMEM((STEPS, planes, rows, levels), jnp.float32),
             pltpu.VMEM((STEPS, planes, rows, levels), jnp.float32),
+            pltpu.VMEM((CUTS[-1] - CUTS[-2],) + pressure.shape[2:], jnp.float32),
             pltpu.SemaphoreType.DMA((7,)),
             pltpu.SemaphoreType.DMA((STEPS, 2, CHUNKS)),
             pltpu.SemaphoreType.DMA((STEPS, 2, CHUNKS)),
@@ -271,6 +345,7 @@
             pltpu.SemaphoreType.DMA((STEPS, 2)),
             pltpu.SemaphoreType.DMA((STEPS,)),
             pltpu.SemaphoreType.DMA((STEPS,)),
+            pltpu.SemaphoreType.DMA((4,)),
         ],
         compiler_params=pltpu.CompilerParams(
             collective_id=0, has_side_effects=True, vmem_limit_bytes=48 * 2**20

time: 189 us -> 188 us (level)
  no operation moved by 1% of the time
where the time goes in v3:
time: 188 us
  Pallas kernels  184 us (98%)
  local copies, waits for them, and re-layouts  3.4 us (2%)
    pallas_call x1, Pallas kernels, shards(): pl.pallas_call(kernel, out_shape=pltpu.VMEM(pressure.shape, jnp.float32),...  184 us

profile of v3, /device:TPU:1, one launch (start us, length us, event | category | flops | bytes accessed | tf_op | source)
XLA Modules:
  0.0 187.7 jit_solution(17631801577842454593)
XLA Ops:
  0.0 184.3 %shard_map.37 = f32[4,64,64,128]{3,2,1,0:T(8,128)S(1)} custom-call(f32[4,64,64,128]{3,2,1,0:T(8,128)} %p_in.1, f32[4,64,64,128]{3,2,1,0:T(8,128)} %e_in.1, f32[4,64,64,128]{3,2,1,0:T(8,128)} %c_in.1), custom_call_target="tpu_custom_call" | custom-call | tf_op jit(solution)/shard_map/pallas_call | solution.py:329
  184.3 3.4 %copy.5 = f32[4,64,64,128]{3,2,1,0:T(8,128)} copy(f32[4,64,64,128]{3,2,1,0:T(8,128)S(1)} %shard_map.37) | data formatting | bytes 16777216

commit v4 on v3

--- a/solution.py
+++ b/solution.py
@@ -6,10 +6,10 @@
 from jax.sharding import PartitionSpec as P
 
 STEPS = 4
-CUTS = (0, 28, 56, 64)
+CUTS = (0, 30, 60, 64)
 CHUNKS = len(CUTS) - 1
 RING = 4
-RELIEF = 2
+RELIEF = 3
 MESH = pl.DeviceIdType.MESH
 
 
@@ -38,7 +38,7 @@
 
     def hop(side, relay, count):
         return pltpu.make_async_remote_copy(
-            src_ref=field[0].at[(1, planes)[side], pl.ds(1 + rows - count, count)],
+            src_ref=field[0].at[(1, planes)[side], pl.ds(1 + CUTS[2] - count, count)],
             dst_ref=passed.at[pl.ds(0, count)],
             send_sem=hop_sem.at[0],
             recv_sem=hop_sem.at[1],
@@ -49,7 +49,7 @@
     def forward(side, dest, count):
         return pltpu.make_async_remote_copy(
             src_ref=passed.at[pl.ds(0, count)],
-            dst_ref=field[0].at[(planes + 1, 0)[side], pl.ds(1 + rows - count, count)],
+            dst_ref=field[0].at[(planes + 1, 0)[side], pl.ds(1 + CUTS[2] - count, count)],
             send_sem=hop_sem.at[2],
             recv_sem=hop_sem.at[3],
             device_id={"lat": dest},
@@ -81,8 +81,8 @@
         )
 
     def sending(t, chunk, action):
-        detoured = t == 0 and chunk == CHUNKS - 1
-        for side in (0, 1):
+        detoured = t == 0 and chunk == 1
+        for side in (1, 0):
             direct = y_has[side]
             if detoured:
                 direct = direct & jnp.logical_not(wraps[side])
@@ -95,7 +95,7 @@
                 action(hop(side, relay, count))
 
     def arriving(t, side, chunk):
-        detoured = t == 0 and chunk == CHUNKS - 1
+        detoured = t == 0 and chunk == 1
         direct = y_has[side]
         if detoured:
             direct = direct & jnp.logical_not(wraps[side])
@@ -337,7 +337,7 @@
             pltpu.VMEM(pressure.shape, jnp.float32),
             pltpu.VMEM((STEPS, planes, rows, levels), jnp.float32),
             pltpu.VMEM((STEPS, planes, rows, levels), jnp.float32),
-            pltpu.VMEM((CUTS[-1] - CUTS[-2],) + pressure.shape[2:], jnp.float32),
+            pltpu.VMEM((RING * RELIEF,) + pressure.shape[2:], jnp.float32),
             pltpu.SemaphoreType.DMA((7,)),
             pltpu.SemaphoreType.DMA((STEPS, 2, CHUNKS)),
             pltpu.SemaphoreType.DMA((STEPS, 2, CHUNKS)),

time: 188 us -> 188 us (level)
  no operation moved by 1% of the time
where the time goes in v4:
time: 188 us
  Pallas kernels  184 us (98%)
  local copies, waits for them, and re-layouts  3.4 us (2%)
    pallas_call x1, Pallas kernels, shards(): pl.pallas_call(kernel, out_shape=pltpu.VMEM(pressure.shape, jnp.float32),...  184 us

profile of v4, /device:TPU:1, one launch (start us, length us, event | category | flops | bytes accessed | tf_op | source)
XLA Modules:
  0.0 187.8 jit_solution(12040419834883619500)
XLA Ops:
  0.0 184.4 %shard_map.37 = f32[4,64,64,128]{3,2,1,0:T(8,128)S(1)} custom-call(f32[4,64,64,128]{3,2,1,0:T(8,128)} %p_in.1, f32[4,64,64,128]{3,2,1,0:T(8,128)} %e_in.1, f32[4,64,64,128]{3,2,1,0:T(8,128)} %c_in.1), custom_call_target="tpu_custom_call" | custom-call | tf_op jit(solution)/shard_map/pallas_call | solution.py:329
  184.4 3.4 %copy.5 = f32[4,64,64,128]{3,2,1,0:T(8,128)} copy(f32[4,64,64,128]{3,2,1,0:T(8,128)S(1)} %shard_map.37) | data formatting | bytes 16777216

commit v5 on v4

--- a/solution.py
+++ b/solution.py
@@ -6,8 +6,10 @@
 from jax.sharding import PartitionSpec as P
 
 STEPS = 4
-CUTS = (0, 30, 60, 64)
+CUTS = (0, 32, 64)
+LAST_CUTS = (0, 32, 60, 64)
 CHUNKS = len(CUTS) - 1
+LAST_CHUNKS = len(LAST_CUTS) - 1
 RING = 4
 RELIEF = 3
 MESH = pl.DeviceIdType.MESH
@@ -56,13 +58,14 @@
             device_id_type=MESH,
         )
 
-    def y_rows(chunk, less=0):
-        return pl.ds(1 + CUTS[chunk], CUTS[chunk + 1] - CUTS[chunk] - less)
+    def y_rows(t, chunk, less=0):
+        cuts = LAST_CUTS if t == STEPS - 1 else CUTS
+        return pl.ds(1 + cuts[chunk], cuts[chunk + 1] - cuts[chunk] - less)
 
     def y_start(t, side, chunk, less=0):
         return pltpu.make_async_remote_copy(
-            src_ref=field[t % 2].at[(1, planes)[side], y_rows(chunk, less)],
-            dst_ref=field[t % 2].at[(planes + 1, 0)[side], y_rows(chunk, less)],
+            src_ref=field[t % 2].at[(1, planes)[side], y_rows(t, chunk, less)],
+            dst_ref=field[t % 2].at[(planes + 1, 0)[side], y_rows(t, chunk, less)],
             send_sem=y_send.at[t, side, chunk],
             recv_sem=y_recv.at[t, 1 - side, chunk],
             device_id=y_to[side],
@@ -70,7 +73,7 @@
         )
 
     def y_arrival(t, side, chunk, less=0):
-        halo = field[t % 2].at[(0, planes + 1)[side], y_rows(chunk, less)]
+        halo = field[t % 2].at[(0, planes + 1)[side], y_rows(t, chunk, less)]
         return pltpu.make_async_remote_copy(
             src_ref=halo,
             dst_ref=halo,
@@ -294,6 +297,9 @@
 
             lax.fori_loop(CUTS[chunk], CUTS[chunk + 1], one, 0)
             sending(t + 1, chunk, lambda copy: copy.start())
+            if t + 1 == STEPS - 1 and chunk == CHUNKS - 1:
+                for piece in range(CHUNKS, LAST_CHUNKS):
+                    sending(t + 1, piece, lambda copy: copy.start())
 
         on_sides(x_has, lambda side: x_start(t + 1, side).start())
         z_copy(t + 1).start()
@@ -307,6 +313,7 @@
 
     for chunk in range(CHUNKS):
         sending(t - 1, chunk, lambda copy: copy.wait_send())
+    for chunk in range(LAST_CHUNKS):
 
         def add(side):
             y_arrival(t, side, chunk).wait_recv()
@@ -317,7 +324,7 @@
                 out[plane, row] = out[plane, row] + c[plane, row] * halo
                 return carry
 
-            lax.fori_loop(CUTS[chunk], CUTS[chunk + 1], one, 0, unroll=4)
+            lax.fori_loop(LAST_CUTS[chunk], LAST_CUTS[chunk + 1], one, 0, unroll=4)
 
         on_sides(y_has, add)
         sending(t, chunk, lambda copy: copy.wait_send())
@@ -339,8 +346,8 @@
             pltpu.VMEM((STEPS, planes, rows, levels), jnp.float32),
             pltpu.VMEM((RING * RELIEF,) + pressure.shape[2:], jnp.float32),
             pltpu.SemaphoreType.DMA((7,)),
-            pltpu.SemaphoreType.DMA((STEPS, 2, CHUNKS)),
-            pltpu.SemaphoreType.DMA((STEPS, 2, CHUNKS)),
+            pltpu.SemaphoreType.DMA((STEPS, 2, LAST_CHUNKS)),
+            pltpu.SemaphoreType.DMA((STEPS, 2, LAST_CHUNKS)),
             pltpu.SemaphoreType.DMA((STEPS, 2)),
             pltpu.SemaphoreType.DMA((STEPS, 2)),
             pltpu.SemaphoreType.DMA((STEPS,)),

time: 188 us -> 188 us (level)
  no operation moved by 1% of the time
where the time goes in v5:
time: 188 us
  Pallas kernels  184 us (98%)
  local copies, waits for them, and re-layouts  3.4 us (2%)
    pallas_call x1, Pallas kernels, shards(): pl.pallas_call(kernel, out_shape=pltpu.VMEM(pressure.shape, jnp.float32),...  184 us

profile of v5, /device:TPU:1, one launch (start us, length us, event | category | flops | bytes accessed | tf_op | source)
XLA Modules:
  0.0 187.9 jit_solution(10450193803673267117)
XLA Ops:
  0.0 184.4 %shard_map.37 = f32[4,64,64,128]{3,2,1,0:T(8,128)S(1)} custom-call(f32[4,64,64,128]{3,2,1,0:T(8,128)} %p_in.1, f32[4,64,64,128]{3,2,1,0:T(8,128)} %e_in.1, f32[4,64,64,128]{3,2,1,0:T(8,128)} %c_in.1), custom_call_target="tpu_custom_call" | custom-call | tf_op jit(solution)/shard_map/pallas_call | solution.py:336
  184.5 3.4 %copy.5 = f32[4,64,64,128]{3,2,1,0:T(8,128)} copy(f32[4,64,64,128]{3,2,1,0:T(8,128)S(1)} %shard_map.37) | data formatting | bytes 16777216

commit v6 on v5

--- a/solution.py
+++ b/solution.py
@@ -326,8 +326,8 @@
 
             lax.fori_loop(LAST_CUTS[chunk], LAST_CUTS[chunk + 1], one, 0, unroll=4)
 
+        sending(t, chunk, lambda copy: copy.wait_send())
         on_sides(y_has, add)
-        sending(t, chunk, lambda copy: copy.wait_send())
 
 
 def shards(pressure, earlier, speed_square):

time: 188 us -> 188 us (level)
  no operation moved by 1% of the time
where the time goes in v6:
time: 188 us
  Pallas kernels  184 us (98%)
  local copies, waits for them, and re-layouts  3.4 us (2%)
    pallas_call x1, Pallas kernels, shards(): pl.pallas_call(kernel, out_shape=pltpu.VMEM(pressure.shape, jnp.float32),...  184 us

profile of v6, /device:TPU:1, one launch (start us, length us, event | category | flops | bytes accessed | tf_op | source)
XLA Modules:
  0.0 187.9 jit_solution(3125956507105756895)
XLA Ops:
  0.0 184.4 %shard_map.37 = f32[4,64,64,128]{3,2,1,0:T(8,128)S(1)} custom-call(f32[4,64,64,128]{3,2,1,0:T(8,128)} %p_in.1, f32[4,64,64,128]{3,2,1,0:T(8,128)} %e_in.1, f32[4,64,64,128]{3,2,1,0:T(8,128)} %c_in.1), custom_call_target="tpu_custom_call" | custom-call | tf_op jit(solution)/shard_map/pallas_call | solution.py:336
  184.5 3.4 %copy.5 = f32[4,64,64,128]{3,2,1,0:T(8,128)} copy(f32[4,64,64,128]{3,2,1,0:T(8,128)S(1)} %shard_map.37) | data formatting | bytes 16777216
